TPU v7x, 256 devices: a whole 4x4x8 slice. The times are simulated.
256 devices in a mesh: row: 32 (over z, x), col: 8 (over y, core).
Axes of the slice: x: 4, y: 4, z: 8, core: 2. Of those that a mesh axis runs over, the one named last changes fastest.
Arguments:
- slab: float32 [16384, 4096], P('row', 'col'), may hold values from -32 to 32, as said below
Outputs:
- factored: float32 [16384, 4096], P('row', 'col')
Inputs may be any that keep to these rules, and one draw needn't show every extreme that they name: The slab holds the first 4096 columns of a symmetric positive definite matrix of order 16384, column blocks of 256 in the stored order of the first step.
All inputs are finite; a program needn't handle non-finite values.
Results may differ from a plain program's by a relative error of at most 0.00029.
Values sent between devices are 32-bit elements; how exact they have to be, the bound alone decides.
A program may use at most 128 MiB of HBM per device.

v0:
```python
import jax
import jax.numpy as jnp
from jax import lax
from jax.sharding import Mesh
from jax.sharding import PartitionSpec as P

BLOCK = 256
PANELS = 2
ROW = ("row_0", "row_1")


PRECISE = lax.Precision.HIGHEST


def broadcast_by_axis(x, axes, root):
    x = jnp.where(lax.axis_index(axes) == root, x, jnp.zeros_like(x))
    for axis in axes:
        x = lax.psum(x, axis)
    return x


def picked(x, axis, root):
    return lax.dynamic_index_in_dim(lax.all_gather(x, axis), root, 0, keepdims=False)


def product(left_side, right_side):
    return jnp.dot(left_side, right_side, precision=PRECISE, preferred_element_type=jnp.float32)


def shards(slab):
    row_count, local_width = slab.shape
    col_count = lax.axis_size("col")
    row_index = lax.axis_index(ROW)
    col_index = lax.axis_index("col")
    blocks_here = local_width // BLOCK
    row_ids = row_index * row_count + jnp.arange(row_count, dtype=jnp.int32)
    global_ids = jnp.arange(blocks_here, dtype=jnp.int32) * col_count + col_index
    identity = jnp.eye(BLOCK, dtype=jnp.float32)
    state = slab
    previous = None
    for sub_step in range(2 * PANELS):
        start = sub_step * BLOCK
        stop = start + BLOCK
        owner_col = sub_step % col_count
        local_block = sub_step // col_count
        home_row = start // row_count
        offset = start % row_count
        first_col = local_block * BLOCK
        column_old = state[:, first_col : first_col + BLOCK]
        diag_tile = column_old[offset : offset + BLOCK]
        if sub_step % 2 == 1:
            cross_tile = previous[offset : offset + BLOCK]
        else:
            cross_tile = jnp.zeros((BLOCK, BLOCK), jnp.float32)
        diag_tile, cross_tile = (
            broadcast_by_axis(diag_tile, ROW, home_row),
            broadcast_by_axis(cross_tile, ROW, home_row),
        )
        column = column_old
        if sub_step % 2 == 1:
            diag_tile = diag_tile - product(cross_tile, cross_tile.T)
            column = column - product(previous, cross_tile.T)
        lower_factor = jnp.linalg.cholesky(diag_tile)
        inverse = jax.scipy.linalg.solve_triangular(lower_factor, identity, lower=True)
        factor = product(column, inverse.T)
        factor = jnp.where(row_ids[:, None] < start, jnp.float32(0.0), factor)
        factor = factor.at[offset : offset + BLOCK].set(
            jnp.where(row_index == home_row, lower_factor, factor[offset : offset + BLOCK])
        )
        state = state.at[:, first_col : first_col + BLOCK].set(
            jnp.where(col_index == owner_col, factor, column_old)
        )
        column_piece = picked(factor, "col", owner_col)
        if sub_step % 2 == 1:
            panel_left = jnp.concatenate([previous, column_piece], axis=1)
            fetched_list = []
            for column_slot in range(blocks_here):
                first_row = (column_slot * col_count + col_index) * BLOCK
                source_row = first_row // row_count
                within = first_row % row_count
                rows_part = lax.dynamic_slice_in_dim(panel_left, within, BLOCK, 0)
                fetched_list.append(broadcast_by_axis(rows_part, ROW, source_row))
            mirrored = jnp.stack(fetched_list, axis=0)
            blocks = state.reshape(row_count, blocks_here, BLOCK)
            change = jnp.einsum("rp,kcp->rkc", panel_left, mirrored, precision=PRECISE)
            keep_mask = (row_ids[:, None, None] >= stop) & (global_ids[None, :, None] > sub_step)
            blocks = jnp.where(keep_mask, blocks - change, blocks)
            state = blocks.reshape(row_count, local_width)
        previous = column_piece
    return state


def solution(mesh):
    split = Mesh(mesh.devices.reshape(8, 4, mesh.shape["col"]), ("row_0", "row_1", "col"))
    in_specs = (P(ROW, "col"),)
    out_specs = P(ROW, "col")
    return jax.shard_map(
        shards, mesh=split, in_specs=in_specs, out_specs=out_specs, check_vma=False
    )
```

profile of v0, /device:TPU:158, one launch (start us, length us, event | category | flops | bytes accessed | tf_op | source)
XLA Modules:
  0.0 1195.7 jit_solution(12574639039874066215)
XLA Ops:
  8.7 72.2 %all-reduce.22.cloned.1.call-done = f32[256,256]{0,1:T(8,128)} async-done(((f32[256,256]{0,1:T(8,128)}), f32[256,256]{0,1:T(8,128)}) %all-reduce.22.cloned.1.call-update) | async-done | bytes 262160 | tf_op jit(solution)/shard_map/psum | solution.py:18
  81.1 49.3 %all-reduce.24.cloned.1.call-done = f32[256,256]{0,1:T(8,128)} async-done(((f32[256,256]{0,1:T(8,128)}), f32[256,256]{0,1:T(8,128)}) %all-reduce.24.cloned.1.call-update) | async-done | bytes 262160 | tf_op jit(solution)/shard_map/psum | solution.py:18
  132.5 11.7 cholesky.214
  144.4 9.8 custom-call.17
  154.8 11.7 cholesky.231
  173.4 19.7 %custom-call.18 = f32[2,128,128]{1,2,0:T(8,128)S(1)} custom-call(f32[2,128,128]{2,1,0:T(8,128)S(1)} %get-tuple-element.129), custom_call_target="InvertDiagBlocksLowerTriangular" | custom-call | tf_op jit(solution)/shard_map/jit(_solve_triangular)/triangular_solve | solution.py:64
  197.9 32.2 %all-gather.9.cloned.1.call-done = f32[4096,256]{0,1:T(8,128)} async-done(((f32[512,256]{0,1:T(8,128)}), f32[4096,256]{0,1:T(8,128)}) %all-gather.9.cloned.1.call-update) | async-done | bytes 4194320 | tf_op jit(solution)/shard_map/all_gather | solution.py:23
  237.1 72.9 %all-reduce.36.cloned.1.call-done = (f32[256,256]{0,1:T(8,128)}, f32[256,256]{0,1:T(8,128)}) async-done(((f32[256,256]{0,1:T(8,128)}, f32[256,256]{0,1:T(8,128)}), (f32[256,256]{0,1:T(8,128)}, f32[256,256]{0,1:T(8,128)})) %all-reduce.36.cloned.1.call-update) | async-done | bytes 524304 | tf_op jit(solution)/shard_map/psum | solution.py:18
  310.3 50.6 %all-reduce.44.cloned.1.call-done = (f32[256,256]{0,1:T(8,128)}, f32[256,256]{0,1:T(8,128)}) async-done(((f32[256,256]{0,1:T(8,128)}, f32[256,256]{0,1:T(8,128)}), (f32[256,256]{0,1:T(8,128)}, f32[256,256]{0,1:T(8,128)})) %all-reduce.44.cloned.1.call-update) | async-done | bytes 524304 | tf_op jit(solution)/shard_map/psum | solution.py:18
  362.9 11.7 cholesky.248
  374.7 9.8 custom-call.19
  385.2 11.7 cholesky.265
  404.6 19.7 %custom-call.20 = f32[2,128,128]{1,2,0:T(8,128)S(1)} custom-call(f32[2,128,128]{2,1,0:T(8,128)S(1)} %get-tuple-element.130), custom_call_target="InvertDiagBlocksLowerTriangular" | custom-call | tf_op jit(solution)/shard_map/jit(_solve_triangular)/triangular_solve | solution.py:64
  429.8 33.3 %all-gather.11.cloned.1.call-done = f32[4096,256]{0,1:T(8,128)} async-done(((f32[512,256]{0,1:T(8,128)}), f32[4096,256]{0,1:T(8,128)}) %all-gather.11.cloned.1.call-update) | async-done | bytes 4194320 | tf_op jit(solution)/shard_map/all_gather | solution.py:23
  465.3 75.4 %all-reduce.34.cloned.1.call-done = (f32[256,512]{0,1:T(8,128)}, f32[256,512]{0,1:T(8,128)}) async-done(((f32[256,512]{0,1:T(8,128)}, f32[256,512]{0,1:T(8,128)}), (f32[256,512]{0,1:T(8,128)}, f32[256,512]{0,1:T(8,128)})) %all-reduce.34.cloned.1.call-update) | async-done | bytes 1048592 | tf_op jit(solution)/shard_map/psum | solution.py:18
  546.1 48.9 %all-reduce.42.cloned.1.call-done = (f32[1,256,512]{1,2,0:T(8,128)}, f32[1,256,512]{1,2,0:T(8,128)}) async-done(((f32[1,256,512]{1,2,0:T(8,128)}, f32[1,256,512]{1,2,0:T(8,128)}), (f32[1,256,512]{1,2,0:T(8,128)}, f32[1,256,512]{1,2,0:T(8,128)})) %all-reduce.42.cloned.1.call-update) | async-done | bytes 1048592 | tf_op jit(solution)/shard_map/psum | solution.py:18
  598.8 71.7 %all-reduce.26.cloned.1.call-done = f32[256,256]{0,1:T(8,128)} async-done(((f32[256,256]{0,1:T(8,128)}), f32[256,256]{0,1:T(8,128)}) %all-reduce.26.cloned.1.call-update) | async-done | bytes 262160 | tf_op jit(solution)/shard_map/psum | solution.py:18
  671.0 48.8 %all-reduce.28.cloned.1.call-done = f32[256,256]{0,1:T(8,128)} async-done(((f32[256,256]{0,1:T(8,128)}), f32[256,256]{0,1:T(8,128)}) %all-reduce.28.cloned.1.call-update) | async-done | bytes 262160 | tf_op jit(solution)/shard_map/psum | solution.py:18
  721.9 11.7 cholesky.282
  733.8 9.8 custom-call.21
  744.2 11.7 cholesky.299
  763.1 19.7 %custom-call.22 = f32[2,128,128]{1,2,0:T(8,128)S(1)} custom-call(f32[2,128,128]{2,1,0:T(8,128)S(1)} %get-tuple-element.131), custom_call_target="InvertDiagBlocksLowerTriangular" | custom-call | tf_op jit(solution)/shard_map/jit(_solve_triangular)/triangular_solve | solution.py:64
  786.8 32.9 %all-gather.13.cloned.1.call-done = f32[4096,256]{0,1:T(8,128)} async-done(((f32[512,256]{0,1:T(8,128)}), f32[4096,256]{0,1:T(8,128)}) %all-gather.13.cloned.1.call-update) | async-done | bytes 4194320 | tf_op jit(solution)/shard_map/all_gather | solution.py:23
  826.8 72.9 %all-reduce.32.cloned.1.call-done = (f32[256,256]{0,1:T(8,128)}, f32[256,256]{0,1:T(8,128)}) async-done(((f32[256,256]{0,1:T(8,128)}, f32[256,256]{0,1:T(8,128)}), (f32[256,256]{0,1:T(8,128)}, f32[256,256]{0,1:T(8,128)})) %all-reduce.32.cloned.1.call-update) | async-done | bytes 524304 | tf_op jit(solution)/shard_map/psum | solution.py:18
  900.0 50.8 %all-reduce.40.cloned.1.call-done = (f32[256,256]{0,1:T(8,128)}, f32[256,256]{0,1:T(8,128)}) async-done(((f32[256,256]{0,1:T(8,128)}, f32[256,256]{0,1:T(8,128)}), (f32[256,256]{0,1:T(8,128)}, f32[256,256]{0,1:T(8,128)})) %all-reduce.40.cloned.1.call-update) | async-done | bytes 524304 | tf_op jit(solution)/shard_map/psum | solution.py:18
  952.7 11.7 cholesky.316
  964.6 9.8 custom-call.23
  975.0 11.7 cholesky.333
  994.2 19.7 %custom-call.24 = f32[2,128,128]{1,2,0:T(8,128)S(1)} custom-call(f32[2,128,128]{2,1,0:T(8,128)S(1)} %get-tuple-element.132), custom_call_target="InvertDiagBlocksLowerTriangular" | custom-call | tf_op jit(solution)/shard_map/jit(_solve_triangular)/triangular_solve | solution.py:64
  1019.3 33.3 %all-gather.15.cloned.1.call-done = f32[4096,256]{0,1:T(8,128)} async-done(((f32[512,256]{0,1:T(8,128)}), f32[4096,256]{0,1:T(8,128)}) %all-gather.15.cloned.1.call-update) | async-done | bytes 4194320 | tf_op jit(solution)/shard_map/all_gather | solution.py:23
  1054.9 75.3 %all-reduce.30.cloned.1.call-done = (f32[256,512]{0,1:T(8,128)}, f32[256,512]{0,1:T(8,128)}) async-done(((f32[256,512]{0,1:T(8,128)}, f32[256,512]{0,1:T(8,128)}), (f32[256,512]{0,1:T(8,128)}, f32[256,512]{0,1:T(8,128)})) %all-reduce.30.cloned.1.call-update) | async-done | bytes 1048592 | tf_op jit(solution)/shard_map/psum | solution.py:18
  1131.0 53.4 %all-reduce.38.cloned.1.call-done = (f32[1,256,512]{1,2,0:T(8,128)}, f32[1,256,512]{1,2,0:T(8,128)}) async-done(((f32[1,256,512]{1,2,0:T(8,128)}, f32[1,256,512]{1,2,0:T(8,128)}), (f32[1,256,512]{1,2,0:T(8,128)}, f32[1,256,512]{1,2,0:T(8,128)})) %all-reduce.38.cloned.1.call-update) | async-done | bytes 1048592 | tf_op jit(solution)/shard_map/psum | solution.py:18
  (222 shorter events, 107.0 us)
Async XLA Ops:
  6.5 74.4 %all-reduce.22.cloned.1.call-start = ((), (), s32[]{:S(2)}) async-start(), calls=%async_computation | async-start | bytes 524288 | tf_op jit(solution)/shard_map/psum | solution.py:18
  8.7 121.8 %all-reduce.24.cloned.1.call-start = ((), (), s32[]{:S(2)}) async-start(), calls=%async_computation.1 | async-start | bytes 524288 | tf_op jit(solution)/shard_map/psum | solution.py:18
  81.0 149.1 %all-gather.9.cloned.1.call-start = ((), (), s32[]{:S(2)}) async-start(), calls=%async_computation.4 | async-start | bytes 4718592 | tf_op jit(solution)/shard_map/all_gather | solution.py:23
  194.8 0.8 copy-start.4
  195.6 114.5 %all-reduce.36.cloned.1.call-start = ((), (), s32[]{:S(2)}) async-start(), calls=%async_computation.11 | async-start | bytes 1048576 | tf_op jit(solution)/shard_map/psum | solution.py:18
  237.1 123.9 %all-reduce.44.cloned.1.call-start = ((), (), s32[]{:S(2)}) async-start(), calls=%async_computation.15 | async-start | bytes 1048576 | tf_op jit(solution)/shard_map/psum | solution.py:18
  310.1 153.0 %all-gather.11.cloned.1.call-start = ((), (), s32[]{:S(2)}) async-start(), calls=%async_computation.5 | async-start | bytes 4718592 | tf_op jit(solution)/shard_map/all_gather | solution.py:23
  360.9 64.3 %copy-start.7 = (f32[256,256]{0,1:T(8,128)S(1)}, f32[256,256]{0,1:T(8,128)}, u32[]{:S(2)}) copy-start(f32[256,256]{0,1:T(8,128)} %get-tuple-element.195) | copy-start | bytes 786436
  427.7 0.8 copy-start
  428.5 112.1 %all-reduce.34.cloned.1.call-start = ((), (), s32[]{:S(2)}) async-start(), calls=%async_computation.10 | async-start | bytes 2097152 | tf_op jit(solution)/shard_map/psum | solution.py:18
  428.6 114.3 %copy-start.1 = (f32[512,256]{0,1:T(8,128)S(1)}, f32[512,256]{0,1:T(8,128)}, u32[]{:S(2)}) copy-start(f32[512,256]{0,1:T(8,128)} %copy-done) | copy-start | bytes 1572868
  465.3 129.7 %all-reduce.42.cloned.1.call-start = ((), (), s32[]{:S(2)}) async-start(), calls=%async_computation.14 | async-start | bytes 2097152 | tf_op jit(solution)/shard_map/psum | solution.py:18
  540.7 129.8 %all-reduce.26.cloned.1.call-start = ((), (), s32[]{:S(2)}) async-start(), calls=%async_computation.2 | async-start | bytes 524288 | tf_op jit(solution)/shard_map/psum | solution.py:18
  598.8 121.1 %all-reduce.28.cloned.1.call-start = ((), (), s32[]{:S(2)}) async-start(), calls=%async_computation.3 | async-start | bytes 524288 | tf_op jit(solution)/shard_map/psum | solution.py:18
  670.6 149.2 %all-gather.13.cloned.1.call-start = ((), (), s32[]{:S(2)}) async-start(), calls=%async_computation.6 | async-start | bytes 4718592 | tf_op jit(solution)/shard_map/all_gather | solution.py:23
  784.4 0.8 copy-start.5
  785.3 114.5 %all-reduce.32.cloned.1.call-start = ((), (), s32[]{:S(2)}) async-start(), calls=%async_computation.9 | async-start | bytes 1048576 | tf_op jit(solution)/shard_map/psum | solution.py:18
  826.8 124.0 %all-reduce.40.cloned.1.call-start = ((), (), s32[]{:S(2)}) async-start(), calls=%async_computation.13 | async-start | bytes 1048576 | tf_op jit(solution)/shard_map/psum | solution.py:18
  899.8 152.8 %all-gather.15.cloned.1.call-start = ((), (), s32[]{:S(2)}) async-start(), calls=%async_computation.7 | async-start | bytes 4718592 | tf_op jit(solution)/shard_map/all_gather | solution.py:23
  950.8 64.0 %copy-start.6 = (f32[256,256]{0,1:T(8,128)S(1)}, f32[256,256]{0,1:T(8,128)}, u32[]{:S(2)}) copy-start(f32[256,256]{0,1:T(8,128)} %get-tuple-element.191) | copy-start | bytes 786436
  1017.2 0.8 copy-start.2
  1018.1 112.3 %copy-start.3 = (f32[512,256]{0,1:T(8,128)S(1)}, f32[512,256]{0,1:T(8,128)}, u32[]{:S(2)}) copy-start(f32[512,256]{0,1:T(8,128)} %copy-done.2) | copy-start | bytes 1572868
  1018.1 112.1 %all-reduce.30.cloned.1.call-start = ((), (), s32[]{:S(2)}) async-start(), calls=%async_computation.8 | async-start | bytes 2097152 | tf_op jit(solution)/shard_map/psum | solution.py:18
  1054.8 129.5 %all-reduce.38.cloned.1.call-start = ((), (), s32[]{:S(2)}) async-start(), calls=%async_computation.12 | async-start | bytes 2097152 | tf_op jit(solution)/shard_map/psum | solution.py:18
Sparse Core Ops, SparseCore 0:
  9.6 71.2 all-reduce.21
  83.3 47.0 all-reduce.23
  195.7 34.3 all-gather.8
  237.2 72.8 all-reduce.35
  312.3 48.5 all-reduce.43
  428.6 34.3 all-gather.10
  465.4 75.1 all-reduce.33
  543.1 51.8 all-reduce.41
  598.9 71.5 all-reduce.25
  672.7 47.0 all-reduce.27
  785.4 34.3 all-gather.12
  826.9 72.8 all-reduce.31
  902.2 48.5 all-reduce.39
  1018.2 34.3 all-gather.14
  1055.0 75.1 all-reduce.29
  1132.5 51.8 all-reduce.37
where the time goes:
time: 1210 us; the launch traced here: 1200 us
  waiting for transfers between devices  874 us (72%)
  other arithmetic  229 us (19%)
  local copies, waits for them, and re-layouts  47.9 us (4%)
  matrix products  21.6 us (2%)
  between operations  19.9 us (2%)
    psum x12, waiting for transfers between devices, broadcast_by_axis(): x = lax.psum(x, axis)  742 us
    another operation x27, other arithmetic, shards(): lower_factor = jnp.linalg.cholesky(diag_tile)  138 us
    all_gather x4, waiting for transfers between devices, picked(): lax.all_gather(x, axis)  132 us
    another operation x9, other arithmetic, shards(): jax.scipy.linalg.solve_triangular(lower_factor, identity, lower=True)  78.8 us
  transfers between devices with their start and end apart: 16, of which 16 were waited for; matrix products, arithmetic and copies ran while one was open for 1% of the time, Pallas kernels for 0%

commit v1 on v0

v1 whole, which is shorter than its diff:
```python
import functools

import jax
import jax.numpy as jnp
from jax import lax
from jax.experimental import pallas as pl
from jax.experimental.pallas import tpu as pltpu
from jax.sharding import PartitionSpec as P

F32, BF16 = jnp.float32, jnp.bfloat16
NN = (((1,), (0,)), ((), ()))
NT = (((1,), (1,)), ((), ()))
TN = (((0,), (0,)), ((), ()))
MESH = pl.DeviceIdType.MESH
TILE = 32
HALF = 128
BLOCK = 256
SIDE = 4 * BLOCK
STRIP = 512
CUT = 64


def split2(x):
    high = x.astype(BF16)
    return high, (x - high.astype(F32)).astype(BF16)


def split3(x):
    high = x.astype(BF16)
    rest = x - high.astype(F32)
    mid = rest.astype(BF16)
    return high, mid, (rest - mid.astype(F32)).astype(BF16)


def product(left, right, dims):
    def dot(a, b):
        return lax.dot_general(a, b, dims, preferred_element_type=F32)

    return dot(left[0], right[0]) + (dot(left[0], right[1]) + dot(left[1], right[0]))


def tile_step(work, t, carry):
    n = TILE
    groups = n // 8
    a = pl.multiple_of(t * n, n)
    lane = lax.broadcasted_iota(jnp.int32, (8, HALF), 1)
    row = lax.broadcasted_iota(jnp.int32, (8, HALF), 0)
    left = [work[pl.ds(a + 8 * g, 8), 0:HALF] for g in range(groups)]
    right = [work[pl.ds(a + 8 * g, 8), HALF : 2 * HALF] for g in range(groups)]

    def spread(x, i):
        return jnp.broadcast_to(x[i : i + 1, :], (8, HALF))

    columns = {}
    for j in range(n):
        chosen = lane == a + j
        for g in range(j // 8, groups):
            only = jnp.sum(jnp.where(chosen, left[g], 0.0), axis=1, keepdims=True)
            columns[j, g] = jnp.broadcast_to(only, (8, HALF))
    scale = [jnp.zeros((8, HALF), F32) for _ in range(groups)]
    for j in range(n):
        own, at = j // 8, j % 8
        root = lax.rsqrt(spread(columns[j, own], at))
        scale[own] = jnp.where(row == at, root, scale[own])
        inverse = root * root
        factor = {}
        for g in range(own, groups):
            base = jnp.where(row > at, columns[j, g], 0.0) if g == own else columns[j, g]
            factor[g] = base * inverse
        for k in range(j + 1, n):
            other = spread(columns[j, k // 8], k % 8)
            for g in range(k // 8, groups):
                columns[k, g] = columns[k, g] - factor[g] * other
        left_row, right_row = spread(left[own], at), spread(right[own], at)
        for g in range(own, groups):
            left[g] = left[g] - factor[g] * left_row
            right[g] = right[g] - factor[g] * right_row
    for g in range(groups):
        left[g] = jnp.where(lane >= a + 8 * g + row, left[g] * scale[g], 0.0)
        right[g] = right[g] * scale[g]
    upper = jnp.concatenate(left, axis=0)
    both = jnp.concatenate([upper, jnp.concatenate(right, axis=0)], axis=1)
    below = lax.broadcasted_iota(jnp.int32, (n, HALF), 1) >= a + n
    lh, lm, ll = split3(jnp.where(below, upper, 0.0))
    bh, bm, bl = split3(both)
    lefts = jnp.concatenate([lh, lh, lm, lh, ll, lm], axis=0)
    boths = jnp.concatenate([bh, bm, bh, bl, bh, bm], axis=0)
    work[...] = work[...] - lax.dot_general(lefts, boths, TN, preferred_element_type=F32)
    work[pl.ds(a, n), :] = both
    return carry


def inverse_factor(work, tile):
    rows = lax.broadcasted_iota(jnp.int32, (HALF, HALF), 0)
    cols = lax.broadcasted_iota(jnp.int32, (HALF, HALF), 1)
    work[:, 0:HALF] = tile
    work[:, HALF : 2 * HALF] = jnp.where(rows == cols, 1.0, 0.0)
    lax.fori_loop(0, HALF // TILE, functools.partial(tile_step, work), 0)
    return work[:, HALF : 2 * HALF]


class Place:
    def __init__(self):
        self.row = lax.axis_index("row")
        self.col = lax.axis_index("col")
        self.z, self.x = self.row // 4, self.row % 4
        self.y, self.core = self.col // 2, self.col % 2

    def near(self, z=0, x=0, y=0, core=0):
        row = (self.z + z + 8) % 8 * 4 + (self.x + x + 4) % 4
        col = (self.y + y + 4) % 4 * 2 + (self.core + core) % 2
        return row, col


STEPS = dict(
    yu=dict(y=1), yd=dict(y=-1), zu=dict(z=1), zd=dict(z=-1), xu=dict(x=1), xd=dict(x=-1), core=dict(core=1)
)
ORDER = ("yu", "yd", "zu", "zd", "xu", "xd", "core")


def star(at, start, up, down):
    relay = at == 3 - start
    return (
        (at == start) | (relay & (start == 1)),
        (at == start) | (relay & (start == 0)),
    )


def relays(me, ref, sems, slot, conds):
    send, recv = sems
    found = []
    for i, name in enumerate(ORDER):
        if name in conds:
            copy = pltpu.make_async_remote_copy(
                src_ref=ref,
                dst_ref=ref,
                send_sem=send.at[slot, i],
                recv_sem=recv.at[slot],
                device_id=me.near(**STEPS[name]),
                device_id_type=MESH,
            )
            found.append((conds[name], copy))
    return found


def corner_chunk(me, corner, sems, big, m):
    c, part = m // 2, m % 2
    source_row = big // 2
    slot = big * (big + 1) + m
    rows = pl.ds(pl.multiple_of(BLOCK * big + HALF * part, HALF), HALF)
    ref = corner.at[rows, pl.ds(pl.multiple_of(BLOCK * c, BLOCK), BLOCK)]
    start_y = c // 2
    mine = me.core == c % 2
    lane = mine & (me.x == source_row)
    root = lane & (me.z == 0)
    yu, yd = star(me.y, start_y, None, None)
    xu, xd = star(me.x, source_row, None, None)
    conds = dict(
        yu=root & yu,
        yd=root & yd,
        zu=lane & (me.z <= 3),
        zd=lane & ((me.z == 0) | (me.z >= 6)),
        xu=mine & xu,
        xd=mine & xd,
        core=mine,
    )
    local_row = (BLOCK * big + HALF * part) % STRIP
    return ref, slot, conds, root & (me.y == start_y), local_row


def column_chunk(me, columns, sems, h, j):
    slot = 20 + 8 * h + j
    rows = pl.ds(pl.multiple_of(STRIP * h + CUT * j, CUT), CUT)
    ref = columns.at[rows, :]
    lane = me.x == h
    xu, xd = star(me.x, h, None, None)
    conds = dict(zu=lane & (me.z <= 3), zd=lane & ((me.z == 0) | (me.z >= 6)), xu=xu, xd=xd)
    return ref, slot, conds, lane & (me.z == 0), CUT * j


def strip_chunk(me, strip, sems, c, j):
    slot = 36 + 4 * c + j
    rows = pl.ds(pl.multiple_of(HALF * j, HALF), HALF)
    ref = strip.at[rows, pl.ds(pl.multiple_of(BLOCK * c, BLOCK), BLOCK)]
    start_y = c // 2
    mine = me.core == c % 2
    yu, yd = star(me.y, start_y, None, None)
    return ref, slot, dict(yu=mine & yu, yd=mine & yd, core=mine), mine & (me.y == start_y), HALF * j


def load(slab, sems, chunk, height, width):
    ref, slot, conds, local, at = chunk

    @pl.when(local)
    def _():
        rows = pl.ds(pl.multiple_of(at, CUT), height)
        pltpu.make_async_copy(slab.at[rows, 0:width], ref, sems[1].at[slot]).start()


def arrive(me, sems, chunk):
    ref, slot, conds, local, at = chunk
    pltpu.make_async_copy(ref, ref, sems[1].at[slot]).wait()
    for cond, copy in relays(me, ref, sems, slot, conds):
        pl.when(cond)(copy.start)


def finish(me, sems, chunk):
    ref, slot, conds, local, at = chunk
    for cond, copy in relays(me, ref, sems, slot, conds):
        pl.when(cond)(copy.wait_send)


def kernel(
    slab, tile_in, out, corner, strip, columns, work, edge, edge_low, side, side_low, down, down_low, inv, inv_low,
    send, recv,
):
    me = Place()
    sems = (send, recv)
    barrier = pltpu.get_barrier_semaphore()
    for name in ORDER:
        pl.semaphore_signal(barrier, inc=1, device_id=me.near(**STEPS[name]), device_id_type=MESH)
    pl.semaphore_wait(barrier, len(ORDER))

    def each(action):
        for big in range(4):
            lax.fori_loop(0, 2 * big + 2, lambda m, _: action(corner_chunk(me, corner, sems, big, m), HALF, BLOCK) or 0, 0)
        for c in range(4):
            lax.fori_loop(0, 4, lambda j, _: action(strip_chunk(me, strip, sems, c, j), HALF, BLOCK) or 0, 0)
        for h in range(2):
            lax.fori_loop(0, 8, lambda j, _: action(column_chunk(me, columns, sems, h, j), CUT, STRIP) or 0, 0)

    each(lambda chunk, height, width: load(slab, sems, chunk, height, width))
    each(lambda chunk, height, width: arrive(me, sems, chunk))

    def span(i):
        return slice(BLOCK * i, BLOCK * i + BLOCK)

    for big in range(4):
        here = span(big)
        before = slice(0, BLOCK * big)
        for j in range(big):
            rest = corner[here, span(j)]
            if j:
                done = slice(0, BLOCK * j)
                rest = rest - product((edge[here, done], edge_low[here, done]), (edge[span(j), done], edge_low[span(j), done]), NT)
            edge[here, span(j)], edge_low[here, span(j)] = split2(product(split2(rest), (inv[span(j)], inv_low[span(j)]), NT))
        tile = corner[here, here]
        if big:
            row_edge = (edge[here, before], edge_low[here, before])
            tile = tile - product(row_edge, row_edge, NT)
        first = inverse_factor(work, tile[0:HALF, 0:HALF])
        first_parts = split2(first)
        link = product(split2(tile[HALF:, 0:HALF]), first_parts, NT)
        link_parts = split2(link)
        second = inverse_factor(work, tile[HALF:, HALF:] - product(link_parts, link_parts, NT))
        cross = -product(split2(second), split2(product(link_parts, first_parts, NN)), NN)
        whole = jnp.concatenate(
            [
                jnp.concatenate([first, jnp.zeros((HALF, HALF), F32)], axis=1),
                jnp.concatenate([cross, second], axis=1),
            ],
            axis=0,
        )
        inv[here, :], inv_low[here, :] = split2(whole)
        inv_parts = (inv[here], inv_low[here])
        rest = strip[:, here]
        rest_cols = columns[here, :]
        if big:
            rest = rest - product((side[:, before], side_low[:, before]), row_edge, NT)
            rest_cols = rest_cols - product(row_edge, (down[before], down_low[before]), NN)
        rest = product(split2(rest), inv_parts, NT)
        side[:, here], side_low[:, here] = split2(rest)

        @pl.when(me.col == big)
        def _(big=big, rest=rest):
            rows = lax.broadcasted_iota(jnp.int32, (STRIP, BLOCK), 0) + me.row * STRIP
            cols = lax.broadcasted_iota(jnp.int32, (STRIP, BLOCK), 1) + BLOCK * big
            out[:, 0:BLOCK] = jnp.where(cols <= rows, rest, 0.0)

        down[here, :], down_low[here, :] = split2(product(inv_parts, split2(rest_cols), NN))

    result = tile_in[...]
    for panel in range(2):
        part = slice(STRIP * panel, STRIP * panel + STRIP)
        change = product((side[:, part], side_low[:, part]), (down[part], down_low[part]), NN)
        result = jnp.where(me.row > panel, result - change, result)
    out[:, BLOCK:] = result[:, BLOCK:]

    @pl.when(me.col >= 4)
    def _():
        out[:, 0:BLOCK] = result[:, 0:BLOCK]

    each(lambda chunk, height, width: finish(me, sems, chunk))


def shards(slab):
    vmem = pl.BlockSpec(memory_space=pltpu.VMEM)
    return pl.pallas_call(
        kernel,
        out_shape=jax.ShapeDtypeStruct(slab.shape, F32),
        in_specs=[pl.BlockSpec(memory_space=pl.ANY), vmem],
        out_specs=vmem,
        scratch_shapes=[
            pltpu.VMEM((SIDE, SIDE), F32),
            pltpu.VMEM((STRIP, SIDE), F32),
            pltpu.VMEM((SIDE, STRIP), F32),
            pltpu.VMEM((HALF, 2 * HALF), F32),
            pltpu.VMEM((SIDE, SIDE), BF16),
            pltpu.VMEM((SIDE, SIDE), BF16),
            pltpu.VMEM((STRIP, SIDE), BF16),
            pltpu.VMEM((STRIP, SIDE), BF16),
            pltpu.VMEM((SIDE, STRIP), BF16),
            pltpu.VMEM((SIDE, STRIP), BF16),
            pltpu.VMEM((SIDE, BLOCK), BF16),
            pltpu.VMEM((SIDE, BLOCK), BF16),
            pltpu.SemaphoreType.DMA((52, len(ORDER))),
            pltpu.SemaphoreType.DMA((52,)),
        ],
        compiler_params=pltpu.CompilerParams(collective_id=0, has_side_effects=True, vmem_limit_bytes=48 * 2**20),
    )(slab, slab)


def solution(mesh):
    spec = P("row", "col")
    return jax.shard_map(shards, mesh=mesh, in_specs=(spec,), out_specs=spec, check_vma=False)
```

time: 1210 us -> 210 us (0.17); the launches traced: 1200 us -> 210 us
  waiting for transfers between devices: 874 us -> 0 us
  other arithmetic: 229 us -> 0 us
  Pallas kernels: 0 us -> 208 us
  local copies, waits for them, and re-layouts: 47.9 us -> 2.2 us
  matrix products: 21.6 us -> 0 us
  between operations: 19.9 us -> 0.01 us
    psum x12 -> x0, waiting for transfers between devices: 742 us -> none  [broadcast_by_axis(): x = lax.psum(x, axis)]
    another operation x38 -> x0, other arithmetic: 219 us -> none  [the longest x27 138 us: shards(): lower_factor = jnp.linalg.cholesky(diag_tile)]
    pallas_call x0 -> x1, Pallas kernels: none -> 208 us  [shards(): pl.pallas_call(kernel, out_shape=jax.ShapeDtypeStruct(slab.shape, F32), i...]
    all_gather x4 -> x0, waiting for transfers between devices: 132 us -> none  [picked(): lax.all_gather(x, axis)]
    another operation x66 -> x0, local copies, waits for them, and re-layouts: 19 us -> none  [the longest x45 16.9 us: shards(): jax.scipy.linalg.solve_triangular(lower_factor, identity, lower=True)]
    unnamed x24 -> x3, local copies, waits for them, and re-layouts: 18.2 us -> 2.2 us
    dot_general x10 -> x0, matrix products: 15.6 us -> none  [the longest x8 9.45 us: product(): jnp.dot(left_side, right_side, precision=PRECISE, preferred_element_type=...]
  transfers between devices with their start and end apart: 16 -> 0, of which waited for: 16 -> 0; matrix products, arithmetic and copies ran while one was open for 1% -> 0% of each run, Pallas kernels for 0% -> 0%
where the time goes in v1:
time: 210 us
  Pallas kernels  208 us (99%)
  local copies, waits for them, and re-layouts  2.2 us (1%)
    pallas_call x1, Pallas kernels, shards(): pl.pallas_call(kernel, out_shape=jax.ShapeDtypeStruct(slab.shape, F32), i...  208 us

profile of v1, /device:TPU:158, one launch (start us, length us, event | category | flops | bytes accessed | tf_op | source)
XLA Modules:
  0.0 210.0 jit_solution(2825968723413816728)
XLA Ops:
  0.0 0.0 copy-start
  0.0 1.2 copy-done
  1.2 207.8 %shard_map.17 = f32[512,512]{1,0:T(8,128)S(1)} custom-call(f32[512,512]{1,0:T(8,128)S(1)} %copy-done, f32[512,512]{1,0:T(8,128)S(1)} %copy-done), custom_call_target="tpu_custom_call" | custom-call | tf_op jit(solution)/shard_map/pallas_call | solution.py:298
  209.0 1.0 copy.3
Async XLA Ops:
  0.0 1.2 copy-start

commit v2 on v1

v2 whole, which is shorter than its diff:
```python
import functools

import jax
import jax.numpy as jnp
from jax import lax
from jax.experimental import pallas as pl
from jax.experimental.pallas import tpu as pltpu
from jax.sharding import PartitionSpec as P

F32, BF16 = jnp.float32, jnp.bfloat16
NN = (((1,), (0,)), ((), ()))
NT = (((1,), (1,)), ((), ()))
TN = (((0,), (0,)), ((), ()))
MESH = pl.DeviceIdType.MESH
TILE = 32
HALF = 128
BLOCK = 256
SIDE = 4 * BLOCK
STRIP = 512
CUT = 64


def split2(x):
    high = x.astype(BF16)
    return high, (x - high.astype(F32)).astype(BF16)


def split3(x):
    high = x.astype(BF16)
    rest = x - high.astype(F32)
    mid = rest.astype(BF16)
    return high, mid, (rest - mid.astype(F32)).astype(BF16)


def product(left, right, dims):
    def dot(a, b):
        return lax.dot_general(a, b, dims, preferred_element_type=F32)

    return dot(left[0], right[0]) + (dot(left[0], right[1]) + dot(left[1], right[0]))


def tile_step(work, t, carry):
    n = TILE
    groups = n // 8
    a = pl.multiple_of(t * n, n)
    lane = lax.broadcasted_iota(jnp.int32, (8, HALF), 1)
    row = lax.broadcasted_iota(jnp.int32, (8, HALF), 0)
    left = [work[pl.ds(a + 8 * g, 8), 0:HALF] for g in range(groups)]
    right = [work[pl.ds(a + 8 * g, 8), HALF : 2 * HALF] for g in range(groups)]

    def spread(x, i):
        return jnp.broadcast_to(x[i : i + 1, :], (8, HALF))

    columns = {}
    for j in range(n):
        chosen = lane == a + j
        for g in range(j // 8, groups):
            only = jnp.sum(jnp.where(chosen, left[g], 0.0), axis=1, keepdims=True)
            columns[j, g] = jnp.broadcast_to(only, (8, HALF))
    scale = [jnp.zeros((8, HALF), F32) for _ in range(groups)]
    for j in range(n):
        own, at = j // 8, j % 8
        root = lax.rsqrt(spread(columns[j, own], at))
        scale[own] = jnp.where(row == at, root, scale[own])
        inverse = root * root
        factor = {}
        for g in range(own, groups):
            base = jnp.where(row > at, columns[j, g], 0.0) if g == own else columns[j, g]
            factor[g] = base * inverse
        for k in range(j + 1, n):
            other = spread(columns[j, k // 8], k % 8)
            for g in range(k // 8, groups):
                columns[k, g] = columns[k, g] - factor[g] * other
        left_row, right_row = spread(left[own], at), spread(right[own], at)
        for g in range(own, groups):
            left[g] = left[g] - factor[g] * left_row
            right[g] = right[g] - factor[g] * right_row
    for g in range(groups):
        left[g] = jnp.where(lane >= a + 8 * g + row, left[g] * scale[g], 0.0)
        right[g] = right[g] * scale[g]
    upper = jnp.concatenate(left, axis=0)
    both = jnp.concatenate([upper, jnp.concatenate(right, axis=0)], axis=1)
    below = lax.broadcasted_iota(jnp.int32, (n, HALF), 1) >= a + n
    lh, lm, ll = split3(jnp.where(below, upper, 0.0))
    bh, bm, bl = split3(both)
    lefts = jnp.concatenate([lh, lh, lm, lh, ll, lm], axis=0)
    boths = jnp.concatenate([bh, bm, bh, bl, bh, bm], axis=0)
    work[...] = work[...] - lax.dot_general(lefts, boths, TN, preferred_element_type=F32)
    work[pl.ds(a, n), :] = both
    return carry


def inverse_factor(work, tile):
    rows = lax.broadcasted_iota(jnp.int32, (HALF, HALF), 0)
    cols = lax.broadcasted_iota(jnp.int32, (HALF, HALF), 1)
    work[:, 0:HALF] = tile
    work[:, HALF : 2 * HALF] = jnp.where(rows == cols, 1.0, 0.0)
    lax.fori_loop(0, HALF // TILE, functools.partial(tile_step, work), 0)
    return work[:, HALF : 2 * HALF]


class Place:
    def __init__(self):
        self.row = lax.axis_index("row")
        self.col = lax.axis_index("col")
        self.z, self.x = self.row // 4, self.row % 4
        self.y, self.core = self.col // 2, self.col % 2
        self.root = (self.row == 0) & (self.col == 0)

    def near(self, z=0, x=0, y=0, core=0):
        row = (self.z + z + 8) % 8 * 4 + (self.x + x + 4) % 4
        col = (self.y + y + 4) % 4 * 2 + (self.core + core) % 2
        return row, col


STEPS = dict(y1=dict(y=1), ym1=dict(y=-1), z1=dict(z=1), zm1=dict(z=-1), x1=dict(x=1), xm1=dict(x=-1), core=dict(core=1))
ORDER = tuple(STEPS)
STARTS = (16, 28, 36)


def star(at, start):
    gap = (at - start + 4) % 4
    rising = (start == 1) | (start == 2)
    return (gap == 0) | ((gap == 1) & rising), (gap == 0) | ((gap == 3) & (rising == False))


def relays(me, ref, sems, slot, conds):
    send, recv = sems
    for i, name in enumerate(ORDER):
        if name in conds:
            copy = pltpu.make_async_remote_copy(
                src_ref=ref,
                dst_ref=ref,
                send_sem=send.at[slot, i],
                recv_sem=recv.at[slot],
                device_id=me.near(**STEPS[name]),
                device_id_type=MESH,
            )
            yield conds[name], copy


def ends(me, lane):
    return lane & (me.z <= 3), lane & ((me.z == 0) | (me.z >= 6))


def root_chunk(me, ref, slot):
    zu, zd = ends(me, (me.x == 0) & (me.y == 0))
    xu, xd = star(me.x, 0)
    yu, yd = star(me.y, 0)
    conds = dict(z1=zu, zm1=zd, x1=(me.y == 0) & xu, xm1=(me.y == 0) & xd, y1=yu, ym1=yd, core=me.core == 0)
    return ref, slot, conds, me.root, 0


def inverse_chunk(me, invs, big, i):
    rows = pl.ds(pl.multiple_of(BLOCK * big + CUT * i, CUT), CUT)
    return root_chunk(me, invs.at[rows, :], 4 * big + i)


def lower_chunk(me, lower, big, i):
    rows = pl.ds(pl.multiple_of(BLOCK * (big + 1) + CUT * i, CUT), CUT)
    return root_chunk(me, lower.at[rows, BLOCK * big : BLOCK * big + BLOCK], STARTS[big] + i)


def column_chunk(me, columns, h, j):
    slot = 40 + 8 * h + j
    rows = pl.ds(pl.multiple_of(STRIP * h + CUT * j, CUT), CUT)
    lane = me.x == h
    xu, xd = star(me.x, h)
    zu, zd = ends(me, lane)
    return columns.at[rows, :], slot, dict(z1=zu, zm1=zd, x1=xu, xm1=xd), lane & (me.z == 0), CUT * j


def strip_chunk(me, strip, c, j):
    slot = 56 + 4 * c + j
    rows = pl.ds(pl.multiple_of(HALF * j, HALF), HALF)
    ref = strip.at[rows, pl.ds(pl.multiple_of(BLOCK * c, BLOCK), BLOCK)]
    start_y = c // 2
    yu, yd = star(me.y, start_y)
    return ref, slot, dict(core=me.core >= 0, y1=yu, ym1=yd), me.y == start_y, HALF * j


class Traffic:
    def __init__(self, me, slab, lower, invs, strip, columns, sems):
        self.me, self.slab, self.sems = me, slab, sems
        self.lower, self.invs, self.strip, self.columns = lower, invs, strip, columns
        self.h = jnp.where((me.x == 0) | (me.x == 3), 0, 1)

    def load(self, chunk, height, width):
        ref, slot, conds, local, at = chunk

        @pl.when(local)
        def _():
            rows = pl.ds(pl.multiple_of(at, CUT), height)
            pltpu.make_async_copy(self.slab.at[rows, 0:width], ref, self.sems[1].at[slot]).start()

    def wait(self, chunk, *_):
        pltpu.make_async_copy(chunk[0], chunk[0], self.sems[1].at[chunk[1]]).wait()

    def send(self, chunk):
        for cond, copy in relays(self.me, chunk[0], self.sems, chunk[1], chunk[2]):
            pl.when(cond)(copy.start)

    def arrive(self, chunk, *_):
        self.wait(chunk)
        self.send(chunk)

    def begin(self, chunk, *_):
        pl.when(chunk[3])(lambda: self.arrive(chunk))

    def follow(self, chunk, *_):
        pl.when(chunk[3] == False)(lambda: self.arrive(chunk))

    def finish(self, chunk, *_):
        for cond, copy in relays(self.me, chunk[0], self.sems, chunk[1], chunk[2]):
            pl.when(cond)(copy.wait_send)

    def spread(self, chunk):
        @pl.when(self.me.root == False)
        def _():
            self.wait(chunk)
            pl.when(self.me.core == 0)(lambda: self.send(chunk))

    def inverse_spread(self, action, big, start=0, count=4):
        loop(count, lambda i: action(inverse_chunk(self.me, self.invs, big, start + i)))

    def lower_spread(self, action, big):
        if big < 3:
            loop(4 * (3 - big), lambda i: action(lower_chunk(self.me, self.lower, big, i)))

    def finish_root(self, chunk):
        pl.when(self.me.core == 0)(lambda: self.finish(chunk))

    def strip_duty(self, action, j):
        for q in range(2):
            action(strip_chunk(self.me, self.strip, self.me.core + 2 * q, j), HALF, BLOCK)

    def strip_need(self, c):
        @pl.when(self.me.core != c % 2)
        def _():
            loop(4, lambda j: self.wait(strip_chunk(self.me, self.strip, c, j)))

    def column_duty(self, action, j):
        action(column_chunk(self.me, self.columns, self.h, j), CUT, STRIP)

    def column_need(self, big):
        @pl.when(self.h != big // 2)
        def _():
            loop(4, lambda j: self.wait(column_chunk(self.me, self.columns, big // 2, 4 * (big % 2) + j)))

    def strips(self, action):
        loop(4, functools.partial(self.strip_duty, action))

    def columns_part(self, action, start, count):
        loop(count, lambda j: self.column_duty(action, start + j))


def loop(count, body):
    def one(i, carry):
        body(i)
        return carry

    lax.fori_loop(0, count, one, 0)


def blocks_to_root():
    return [(0, 1, 1)] + [(1, c, 2) for c in range(3)] + [(1, c, 3) for c in range(4)]


def span(i):
    return slice(BLOCK * i, BLOCK * i + BLOCK)


def factor_corner(traffic, corner, lower, invs, edge, edge_low, work, ready):
    for big in range(4):
        here = span(big)
        before = slice(0, BLOCK * big)
        for c in range(big + 1):
            ready(big, c)
        tile = corner[here, here]
        if big:
            row_edge = (edge[here, before], edge_low[here, before])
            tile = tile - product(row_edge, row_edge, NT)
        first = inverse_factor(work, tile[0:HALF, 0:HALF])
        first_parts = split2(first)
        top = jnp.concatenate([first, jnp.zeros((HALF, HALF), F32)], axis=1)
        invs[BLOCK * big : BLOCK * big + HALF, :] = top
        link_parts = split2(product(split2(tile[HALF:, 0:HALF]), first_parts, NT))
        traffic.inverse_spread(traffic.send, big, 0, 2)
        second = inverse_factor(work, tile[HALF:, HALF:] - product(link_parts, link_parts, NT))
        cross = -product(split2(second), split2(product(link_parts, first_parts, NN)), NN)
        bottom = jnp.concatenate([cross, second], axis=1)
        invs[BLOCK * big + HALF : BLOCK * big + BLOCK, :] = bottom
        traffic.inverse_spread(traffic.send, big, 2, 2)
        whole = jnp.concatenate([top, bottom], axis=0)
        inv_parts = split2(whole)
        for low in range(big + 1, 4):
            ready(low, big)
            rest = corner[span(low), here]
            if big:
                rest = rest - product((edge[span(low), before], edge_low[span(low), before]), row_edge, NT)
            rest = product(split2(rest), inv_parts, NT)
            lower[span(low), here] = rest
            edge[span(low), here], edge_low[span(low), here] = split2(rest)
        traffic.lower_spread(traffic.send, big)


def kernel(
    slab, out, tile_in, corner, lower, invs, strip, columns, work, edge, edge_low, side, side_low, down, down_low,
    send, recv, gather_send, gather_recv, own_sem,
):
    me = Place()
    traffic = Traffic(me, slab, lower, invs, strip, columns, (send, recv))

    @pl.when(me.root)
    def _():
        pltpu.make_async_copy(slab.at[:, 0:BLOCK], corner.at[0:STRIP, 0:BLOCK], gather_recv.at[0]).start()

    traffic.strips(traffic.load)
    traffic.columns_part(traffic.load, 0, 8)
    own = pltpu.make_async_copy(slab, tile_in, own_sem)
    own.start()
    barrier = pltpu.get_barrier_semaphore()
    for name in ORDER:
        pl.semaphore_signal(barrier, inc=1, device_id=me.near(**STEPS[name]), device_id_type=MESH)
    diagonal = (me.row == 1) & (me.col >= 1) & (me.col < 4)

    @pl.when(me.root)
    def _():
        for c in range(1, 4):
            pl.semaphore_signal(barrier, inc=1, device_id=(1, c), device_id_type=MESH)

    @pl.when(diagonal)
    def _():
        pl.semaphore_signal(barrier, inc=1, device_id=(0, 0), device_id_type=MESH)

    pl.semaphore_wait(barrier, len(ORDER) + jnp.where(me.root, 3, jnp.where(diagonal, 1, 0)))

    def to_root(row, c, big):
        at = BLOCK * big - STRIP * row
        slot = 1 + blocks_to_root().index((row, c, big))
        copy = pltpu.make_async_remote_copy(
            src_ref=slab.at[at : at + BLOCK, 0:BLOCK],
            dst_ref=corner.at[span(big), span(c)],
            send_sem=gather_send.at[slot],
            recv_sem=gather_recv.at[slot],
            device_id=(0, 0),
            device_id_type=MESH,
        )
        return (me.row == row) & (me.col == c), copy

    for block in blocks_to_root():
        sender, copy = to_root(*block)
        pl.when(sender)(copy.start)
    traffic.strips(traffic.begin)
    traffic.columns_part(traffic.begin, 0, 8)

    seen = set()

    def ready(big, c):
        if (big, c) in seen:
            return
        seen.add((big, c))
        if (big, c) == (0, 0):
            pltpu.make_async_copy(slab.at[:, 0:BLOCK], corner.at[0:STRIP, 0:BLOCK], gather_recv.at[0]).wait()
        elif (big, c) != (1, 0):
            to_root(big // 2, c, big)[1].wait_recv()

    @pl.when(me.root)
    def _():
        factor_corner(traffic, corner, lower, invs, edge, edge_low, work, ready)

    traffic.strips(traffic.follow)
    traffic.columns_part(traffic.follow, 0, 4)
    for big in range(4):
        here = span(big)
        before = slice(0, BLOCK * big)
        if big:
            traffic.strip_need(big)
            traffic.column_need(big)
        if big:
            rest = strip[:, here]
            rest_cols = columns[here, :]
            row_edge = split2(lower[here, before])
            rest = rest - product((side[:, before], side_low[:, before]), row_edge, NT)
            rest_cols = rest_cols - product(row_edge, (down[before], down_low[before]), NN)
        traffic.inverse_spread(traffic.spread, big)
        if not big:
            traffic.columns_part(traffic.follow, 4, 2)
            traffic.lower_spread(traffic.spread, 0)
            traffic.columns_part(traffic.follow, 6, 2)
            traffic.strip_need(0)
            traffic.column_need(0)
            own.wait()
            rest = strip[:, here]
            rest_cols = columns[here, :]
        inv_parts = split2(invs[here, :])
        rest = product(split2(rest), inv_parts, NT)
        side[:, here], side_low[:, here] = split2(rest)

        @pl.when(me.col == big)
        def _(big=big, rest=rest):
            rows = lax.broadcasted_iota(jnp.int32, (STRIP, BLOCK), 0) + me.row * STRIP
            cols = lax.broadcasted_iota(jnp.int32, (STRIP, BLOCK), 1) + BLOCK * big
            out[:, 0:BLOCK] = jnp.where(cols <= rows, rest, 0.0)

        down[here, :], down_low[here, :] = split2(product(inv_parts, split2(rest_cols), NN))
        if big:
            traffic.lower_spread(traffic.spread, big)
        change = product((side[:, here], side_low[:, here]), (down[here], down_low[here]), NN)
        tile_in[...] = jnp.where(me.row > big // 2, tile_in[...] - change, tile_in[...])

    result = tile_in
    out[:, BLOCK:] = result[:, BLOCK:]

    @pl.when(me.col >= 4)
    def _():
        out[:, 0:BLOCK] = result[:, 0:BLOCK]

    for big in range(4):
        traffic.inverse_spread(traffic.finish_root, big)
        traffic.lower_spread(traffic.finish_root, big)
    traffic.strips(traffic.finish)
    traffic.columns_part(traffic.finish, 0, 8)
    for block in blocks_to_root():
        sender, copy = to_root(*block)
        pl.when(sender)(copy.wait_send)


def shards(slab):
    vmem = pl.BlockSpec(memory_space=pltpu.VMEM)
    return pl.pallas_call(
        kernel,
        out_shape=jax.ShapeDtypeStruct(slab.shape, F32),
        in_specs=[pl.BlockSpec(memory_space=pl.ANY)],
        out_specs=vmem,
        scratch_shapes=[
            pltpu.VMEM((STRIP, STRIP), F32),
            pltpu.VMEM((SIDE, SIDE), F32),
            pltpu.VMEM((SIDE, SIDE), F32),
            pltpu.VMEM((SIDE, BLOCK), F32),
            pltpu.VMEM((STRIP, SIDE), F32),
            pltpu.VMEM((SIDE, STRIP), F32),
            pltpu.VMEM((HALF, 2 * HALF), F32),
            pltpu.VMEM((SIDE, SIDE), BF16),
            pltpu.VMEM((SIDE, SIDE), BF16),
            pltpu.VMEM((STRIP, SIDE), BF16),
            pltpu.VMEM((STRIP, SIDE), BF16),
            pltpu.VMEM((SIDE, STRIP), BF16),
            pltpu.VMEM((SIDE, STRIP), BF16),
            pltpu.SemaphoreType.DMA((72, len(ORDER))),
            pltpu.SemaphoreType.DMA((72,)),
            pltpu.SemaphoreType.DMA((9,)),
            pltpu.SemaphoreType.DMA((9,)),
            pltpu.SemaphoreType.DMA,
        ],
        compiler_params=pltpu.CompilerParams(collective_id=0, has_side_effects=True, vmem_limit_bytes=48 * 2**20),
    )(slab)


def solution(mesh):
    spec = P("row", "col")
    return jax.shard_map(shards, mesh=mesh, in_specs=(spec,), out_specs=spec, check_vma=False)
```

time: 210 us -> 114 us (0.54)
  the two profiles are of different devices: /device:TPU:158 before, /device:TPU:149 now
where the time goes in v2:
time: 114 us
  Pallas kernels  111 us (97%)
  local copies, waits for them, and re-layouts  2.2 us (2%)
    pallas_call x1, Pallas kernels, shards(): pl.pallas_call(kernel, out_shape=jax.ShapeDtypeStruct(slab.shape, F32), i...  111 us

profile of v2, /device:TPU:149, one launch (start us, length us, event | category | flops | bytes accessed | tf_op | source)
XLA Modules:
  0.0 113.5 jit_solution(13704759820777360728)
XLA Ops:
  0.0 0.0 copy-start
  0.0 1.2 %copy-done = f32[512,512]{1,0:T(8,128)S(1)} copy-done((f32[512,512]{1,0:T(8,128)S(1)}, f32[512,512]{1,0:T(8,128)}, u32[]{:S(2)}) %copy-start) | copy-done | bytes 1048600
  1.2 111.3 %shard_map.17 = f32[512,512]{1,0:T(8,128)S(1)} custom-call(f32[512,512]{1,0:T(8,128)S(1)} %copy-done), custom_call_target="tpu_custom_call" | custom-call | tf_op jit(solution)/shard_map/pallas_call | solution.py:431
  112.5 1.0 copy.3
Async XLA Ops:
  0.0 1.2 %copy-start = (f32[512,512]{1,0:T(8,128)S(1)}, f32[512,512]{1,0:T(8,128)}, u32[]{:S(2)}) copy-start(f32[512,512]{1,0:T(8,128)} %slab.1) | copy-start | bytes 3145732

commit v3 on v2

--- a/solution.py
+++ b/solution.py
@@ -18,6 +18,8 @@
 SIDE = 4 * BLOCK
 STRIP = 512
 CUT = 64
+SLICE = 32
+PER_HALF = STRIP // SLICE
 
 
 def split2(x):
@@ -106,6 +108,20 @@
         self.z, self.x = self.row // 4, self.row % 4
         self.y, self.core = self.col // 2, self.col % 2
         self.root = (self.row == 0) & (self.col == 0)
+        self.peers = {name: self.near(**step) for name, step in STEPS.items()}
+        self.half = jnp.where((self.x == 0) | (self.x == 3), 0, 1)
+        zu, zd = ends(self, (self.x == 0) & (self.y == 0))
+        xu, xd = star(self.x, 0)
+        level = self.y == 0
+        yu, yd = self.y <= 1, level
+        self.root_conds = dict(z1=zu, zm1=zd, x1=level & xu, xm1=level & xd, y1=yu, ym1=yd, core=self.core == 0)
+        xu, xd = star(self.x, self.half)
+        zu, zd = ends(self, self.x == self.half)
+        self.column_conds = dict(z1=zu, zm1=zd, x1=xu, xm1=xd)
+        self.strip_conds = []
+        for start in range(2):
+            yu, yd = star(self.y, start)
+            self.strip_conds.append(dict(core=self.core >= 0, y1=yu, ym1=yd))
 
     def near(self, z=0, x=0, y=0, core=0):
         row = (self.z + z + 8) % 8 * 4 + (self.x + x + 4) % 4
@@ -115,7 +131,7 @@
 
 STEPS = dict(y1=dict(y=1), ym1=dict(y=-1), z1=dict(z=1), zm1=dict(z=-1), x1=dict(x=1), xm1=dict(x=-1), core=dict(core=1))
 ORDER = tuple(STEPS)
-STARTS = (16, 28, 36)
+STARTS = (16, 22, 26)
 
 
 def star(at, start):
@@ -133,7 +149,7 @@
                 dst_ref=ref,
                 send_sem=send.at[slot, i],
                 recv_sem=recv.at[slot],
-                device_id=me.near(**STEPS[name]),
+                device_id=me.peers[name],
                 device_id_type=MESH,
             )
             yield conds[name], copy
@@ -144,11 +160,7 @@
 
 
 def root_chunk(me, ref, slot):
-    zu, zd = ends(me, (me.x == 0) & (me.y == 0))
-    xu, xd = star(me.x, 0)
-    yu, yd = star(me.y, 0)
-    conds = dict(z1=zu, zm1=zd, x1=(me.y == 0) & xu, xm1=(me.y == 0) & xd, y1=yu, ym1=yd, core=me.core == 0)
-    return ref, slot, conds, me.root, 0
+    return ref, slot, me.root_conds, me.root, 0
 
 
 def inverse_chunk(me, invs, big, i):
@@ -157,41 +169,37 @@
 
 
 def lower_chunk(me, lower, big, i):
-    rows = pl.ds(pl.multiple_of(BLOCK * (big + 1) + CUT * i, CUT), CUT)
+    rows = pl.ds(pl.multiple_of(BLOCK * (big + 1) + HALF * i, HALF), HALF)
     return root_chunk(me, lower.at[rows, BLOCK * big : BLOCK * big + BLOCK], STARTS[big] + i)
 
 
-def column_chunk(me, columns, h, j):
-    slot = 40 + 8 * h + j
-    rows = pl.ds(pl.multiple_of(STRIP * h + CUT * j, CUT), CUT)
-    lane = me.x == h
-    xu, xd = star(me.x, h)
-    zu, zd = ends(me, lane)
-    return columns.at[rows, :], slot, dict(z1=zu, zm1=zd, x1=xu, xm1=xd), lane & (me.z == 0), CUT * j
-
-
-def strip_chunk(me, strip, c, j):
-    slot = 56 + 4 * c + j
+def column_chunk(me, columns, h, j, first):
+    slot = 40 + PER_HALF * h + j
+    rows = pl.ds(pl.multiple_of(STRIP * h + SLICE * j, SLICE), SLICE)
+    return columns.at[rows, first:STRIP], slot, me.column_conds, (me.x == h) & (me.z == 0), SLICE * j
+
+
+def strip_chunk(me, strip, start, core, j):
+    c = 2 * start + core
+    slot = 40 + 2 * PER_HALF + 4 * c + j
     rows = pl.ds(pl.multiple_of(HALF * j, HALF), HALF)
     ref = strip.at[rows, pl.ds(pl.multiple_of(BLOCK * c, BLOCK), BLOCK)]
-    start_y = c // 2
-    yu, yd = star(me.y, start_y)
-    return ref, slot, dict(core=me.core >= 0, y1=yu, ym1=yd), me.y == start_y, HALF * j
+    return ref, slot, me.strip_conds[start], me.y == start, HALF * j
 
 
 class Traffic:
     def __init__(self, me, slab, lower, invs, strip, columns, sems):
         self.me, self.slab, self.sems = me, slab, sems
         self.lower, self.invs, self.strip, self.columns = lower, invs, strip, columns
-        self.h = jnp.where((me.x == 0) | (me.x == 3), 0, 1)
-
-    def load(self, chunk, height, width):
+        self.h = me.half
+
+    def load(self, chunk, height, first, last):
         ref, slot, conds, local, at = chunk
 
         @pl.when(local)
         def _():
-            rows = pl.ds(pl.multiple_of(at, CUT), height)
-            pltpu.make_async_copy(self.slab.at[rows, 0:width], ref, self.sems[1].at[slot]).start()
+            rows = pl.ds(pl.multiple_of(at, SLICE), height)
+            pltpu.make_async_copy(self.slab.at[rows, first:last], ref, self.sems[1].at[slot]).start()
 
     def wait(self, chunk, *_):
         pltpu.make_async_copy(chunk[0], chunk[0], self.sems[1].at[chunk[1]]).wait()
@@ -225,33 +233,46 @@
 
     def lower_spread(self, action, big):
         if big < 3:
-            loop(4 * (3 - big), lambda i: action(lower_chunk(self.me, self.lower, big, i)))
+            loop(2 * (3 - big), lambda i: action(lower_chunk(self.me, self.lower, big, i)))
 
     def finish_root(self, chunk):
         pl.when(self.me.core == 0)(lambda: self.finish(chunk))
 
     def strip_duty(self, action, j):
         for q in range(2):
-            action(strip_chunk(self.me, self.strip, self.me.core + 2 * q, j), HALF, BLOCK)
+            action(strip_chunk(self.me, self.strip, q, self.me.core, j), HALF, 0, BLOCK)
 
     def strip_need(self, c):
         @pl.when(self.me.core != c % 2)
         def _():
-            loop(4, lambda j: self.wait(strip_chunk(self.me, self.strip, c, j)))
-
-    def column_duty(self, action, j):
-        action(column_chunk(self.me, self.columns, self.h, j), CUT, STRIP)
+            loop(4, lambda j: self.wait(strip_chunk(self.me, self.strip, c // 2, c % 2, j)))
+
+    def by_width(self, body):
+        pl.when(self.me.y < 2)(lambda: body(BLOCK))
+        pl.when(self.me.y >= 2)(lambda: body(0))
 
     def column_need(self, big):
-        @pl.when(self.h != big // 2)
-        def _():
-            loop(4, lambda j: self.wait(column_chunk(self.me, self.columns, big // 2, 4 * (big % 2) + j)))
+        count = BLOCK // SLICE
+
+        def body(first):
+            loop(
+                count,
+                lambda j: self.wait(column_chunk(self.me, self.columns, big // 2, count * (big % 2) + j, first)),
+            )
+
+        pl.when(self.h != big // 2)(lambda: self.by_width(body))
 
     def strips(self, action):
         loop(4, functools.partial(self.strip_duty, action))
 
     def columns_part(self, action, start, count):
-        loop(count, lambda j: self.column_duty(action, start + j))
+        def body(first):
+            loop(
+                count,
+                lambda j: action(column_chunk(self.me, self.columns, self.h, start + j, first), SLICE, first, STRIP),
+            )
+
+        self.by_width(body)
 
 
 def loop(count, body):
@@ -316,12 +337,17 @@
         pltpu.make_async_copy(slab.at[:, 0:BLOCK], corner.at[0:STRIP, 0:BLOCK], gather_recv.at[0]).start()
 
     traffic.strips(traffic.load)
-    traffic.columns_part(traffic.load, 0, 8)
+    traffic.columns_part(traffic.load, 0, PER_HALF)
+
+    @pl.when(me.y < 2)
+    def _():
+        columns[:, 0:BLOCK] = jnp.zeros((SIDE, BLOCK), F32)
+
     own = pltpu.make_async_copy(slab, tile_in, own_sem)
     own.start()
     barrier = pltpu.get_barrier_semaphore()
     for name in ORDER:
-        pl.semaphore_signal(barrier, inc=1, device_id=me.near(**STEPS[name]), device_id_type=MESH)
+        pl.semaphore_signal(barrier, inc=1, device_id=me.peers[name], device_id_type=MESH)
     diagonal = (me.row == 1) & (me.col >= 1) & (me.col < 4)
 
     @pl.when(me.root)
@@ -352,7 +378,7 @@
         sender, copy = to_root(*block)
         pl.when(sender)(copy.start)
     traffic.strips(traffic.begin)
-    traffic.columns_part(traffic.begin, 0, 8)
+    traffic.columns_part(traffic.begin, 0, PER_HALF)
 
     seen = set()
 
@@ -370,7 +396,7 @@
         factor_corner(traffic, corner, lower, invs, edge, edge_low, work, ready)
 
     traffic.strips(traffic.follow)
-    traffic.columns_part(traffic.follow, 0, 4)
+    traffic.columns_part(traffic.follow, 0, PER_HALF // 2)
     for big in range(4):
         here = span(big)
         before = slice(0, BLOCK * big)
@@ -385,9 +411,9 @@
             rest_cols = rest_cols - product(row_edge, (down[before], down_low[before]), NN)
         traffic.inverse_spread(traffic.spread, big)
         if not big:
-            traffic.columns_part(traffic.follow, 4, 2)
+            traffic.columns_part(traffic.follow, PER_HALF // 2, PER_HALF // 4)
             traffic.lower_spread(traffic.spread, 0)
-            traffic.columns_part(traffic.follow, 6, 2)
+            traffic.columns_part(traffic.follow, 3 * PER_HALF // 4, PER_HALF // 4)
             traffic.strip_need(0)
             traffic.column_need(0)
             own.wait()
@@ -420,7 +446,7 @@
         traffic.inverse_spread(traffic.finish_root, big)
         traffic.lower_spread(traffic.finish_root, big)
     traffic.strips(traffic.finish)
-    traffic.columns_part(traffic.finish, 0, 8)
+    traffic.columns_part(traffic.finish, 0, PER_HALF)
     for block in blocks_to_root():
         sender, copy = to_root(*block)
         pl.when(sender)(copy.wait_send)
@@ -447,8 +473,8 @@
             pltpu.VMEM((STRIP, SIDE), BF16),
             pltpu.VMEM((SIDE, STRIP), BF16),
             pltpu.VMEM((SIDE, STRIP), BF16),
-            pltpu.SemaphoreType.DMA((72, len(ORDER))),
-            pltpu.SemaphoreType.DMA((72,)),
+            pltpu.SemaphoreType.DMA((88, len(ORDER))),
+            pltpu.SemaphoreType.DMA((88,)),
             pltpu.SemaphoreType.DMA((9,)),
             pltpu.SemaphoreType.DMA((9,)),
             pltpu.SemaphoreType.DMA,

time: 114 us -> 96.1 us (0.84)
  the two profiles are of different devices: /device:TPU:149 before, /device:TPU:157 now
where the time goes in v3:
time: 96.1 us; the launch traced here: 96 us
  Pallas kernels  93.8 us (98%)
  local copies, waits for them, and re-layouts  2.2 us (2%)
    pallas_call x1, Pallas kernels, shards(): pl.pallas_call(kernel, out_shape=jax.ShapeDtypeStruct(slab.shape, F32), i...  93.8 us
    unnamed x3, local copies, waits for them, and re-layouts  2.2 us

profile of v3, /device:TPU:157, one launch (start us, length us, event | category | flops | bytes accessed | tf_op | source)
XLA Modules:
  0.0 96.0 jit_solution(12322614838968706393)
XLA Ops:
  0.0 0.0 copy-start
  0.0 1.2 %copy-done = f32[512,512]{1,0:T(8,128)S(1)} copy-done((f32[512,512]{1,0:T(8,128)S(1)}, f32[512,512]{1,0:T(8,128)}, u32[]{:S(2)}) %copy-start) | copy-done | bytes 1048600
  1.2 93.8 %shard_map.17 = f32[512,512]{1,0:T(8,128)S(1)} custom-call(f32[512,512]{1,0:T(8,128)S(1)} %copy-done), custom_call_target="tpu_custom_call" | custom-call | tf_op jit(solution)/shard_map/pallas_call | solution.py:457
  95.0 1.0 %copy.3 = f32[512,512]{1,0:T(8,128)} copy(f32[512,512]{1,0:T(8,128)S(1)} %shard_map.17) | data formatting | bytes 2097152
Async XLA Ops:
  0.0 1.2 %copy-start = (f32[512,512]{1,0:T(8,128)S(1)}, f32[512,512]{1,0:T(8,128)}, u32[]{:S(2)}) copy-start(f32[512,512]{1,0:T(8,128)} %slab.1) | copy-start | bytes 3145732
